TPU v7x, 32 devices: a whole 2x2x4 slice. The times are simulated.
32 devices in a mesh: atom: 8 (over z, x), energy: 4 (over y, core).
Axes of the slice: x: 2, y: 2, z: 4, core: 2. Of those that a mesh axis runs over, the one named last changes fastest.
Arguments:
- t_matrix: float32 [4, 64, 16, 16], P('energy', 'atom'), may hold values from -1.5 to 1.5
- structure: bfloat16 [4, 64, 1024, 1024], P('energy', 'atom'), may hold values from -0.125 to 0.125
- radial: bfloat16 [4, 64, 16, 1024], P('energy', 'atom'), may hold values from -3 to 3
- weights: float32 [4], P('energy'), may hold values from 0.1 to 1
- neighbours: int32 [64, 64], P('atom'), may hold values from 0 to 63, as said below
- live: int32 [64, 64], P('atom'), may hold values from 0 to 1, as said below
Outputs:
- density: float32 [64, 1024], P('atom', 'energy')
Inputs may be any that keep to these rules, and one draw needn't show every extreme that they name: `neighbours`: slot 0 of atom i holds i itself. Atom i lies at index i // 8 of the atom axis, and every neighbour of it lies at an index that differs from that one by at most 3 around the axis, which closes into a loop; both extremes occur in every draw. An atom may appear in several slots of one zone. `live`: each row is 1 on its first slots and 0 after; slot 0 is always 1, at least 16 slots are 1, and some atom has all 64 slots 1.
All inputs are finite; a program needn't handle non-finite values.
Results may differ from a plain program's by a relative error of at most 0.0043.
Values sent between devices are 32-bit elements; how exact they have to be, the bound alone decides.
A program may use at most 128 MiB of HBM per device.

v0:
```python
import functools

import jax
import jax.numpy as jnp
from jax import lax
from jax.experimental import pallas as pl
from jax.experimental.pallas import tpu as pltpu
from jax.sharding import PartitionSpec as P

ITERS = 4
SPAN = 3

NT = (((1,), (1,)), ((), ()))
NN = (((1,), (0,)), ((), ()))


def mm(a, b, dims=NN):
    return lax.dot_general(a, b, dims, preferred_element_type=jnp.float32)


def kernel(
    n_atom, n_energy, a_dev, lm, zone,
    t_hbm, s_hbm, r_hbm, w_hbm, nb_hbm, live_hbm, out_ref,
    t_ref, w_ref, nb_ref, live_ref, s_v, s_t, r_v, t_send, t_all, firstx, table, hot, bd, img, idx_v, idx_s,
    acc, landed, d_mine, d_land,
    s_sem, misc_sem, ts_sem, tr_sem, as_sem, ar_sem, ds_sem, dr_sem,
):
    bf16, f32 = jnp.bfloat16, jnp.float32
    places = 2 * SPAN + 1
    lanes = a_dev * lm
    dim = zone * lm
    n_groups = dim // lanes
    per = lanes // lm
    me = lax.axis_index("atom")
    my_e = lax.axis_index("energy")

    small = [
        pltpu.make_async_copy(source, target, misc_sem.at[2 + n])
        for n, (source, target) in enumerate(
            ((t_hbm, t_ref), (nb_hbm, nb_ref), (live_hbm, live_ref), (w_hbm, w_ref))
        )
    ]
    for copy in small:
        copy.start()
    for a in range(a_dev):
        pltpu.make_async_copy(s_hbm.at[a], s_v.at[a], s_sem.at[a]).start()
    r_copy = pltpu.make_async_copy(r_hbm, r_v, misc_sem.at[0])
    r_copy.start()

    def atom_at(d):
        return lax.rem(me + (d + n_atom), n_atom)

    shifts = [d for d in range(-SPAN, SPAN + 1) if d != 0]
    barrier = pltpu.get_barrier_semaphore()
    for d in shifts:
        pl.semaphore_signal(barrier, inc=1, device_id={"atom": atom_at(d)}, device_id_type=pl.DeviceIdType.MESH)
    for d in range(1, n_energy):
        pl.semaphore_signal(
            barrier, inc=1, device_id={"energy": lax.rem(my_e + d, n_energy)}, device_id_type=pl.DeviceIdType.MESH
        )

    for copy in small:
        copy.wait()
    t_turned = jnp.transpose(t_ref[...])
    t_send[...] = t_turned
    ids = nb_ref[...] - (me - SPAN) * a_dev
    total = n_atom * a_dev
    ids = jnp.where(ids < 0, ids + total, ids)
    ids = jnp.where(ids >= total, ids - total, ids)
    idx_v[...] = jnp.where(live_ref[...] > 0, ids, places * a_dev)
    i_copy = pltpu.make_async_copy(idx_v, idx_s, misc_sem.at[1])
    i_copy.start()

    pl.semaphore_wait(barrier, len(shifts) + n_energy - 1)

    def send_t(d):
        return pltpu.make_async_remote_copy(
            src_ref=t_send, dst_ref=t_all.at[SPAN - d], send_sem=ts_sem.at[SPAN - d],
            recv_sem=tr_sem.at[SPAN - d], device_id={"atom": atom_at(d)}, device_id_type=pl.DeviceIdType.MESH,
        )

    t_copies = [send_t(d) for d in shifts]
    for copy in t_copies:
        copy.start()

    lane16 = lax.broadcasted_iota(jnp.int32, (lm, lanes), 1)
    for a in range(a_dev):
        moved = t_turned if a == 0 else pltpu.roll(t_turned, lanes - a * lm, 1)
        firstx[a] = jnp.where(lane16 < lm, moved, 0.0)

    wide = lax.broadcasted_iota(jnp.int32, (lm, places * lanes), 1)
    tall = lax.broadcasted_iota(jnp.int32, (lm, places * lanes), 0)

    order = [p for d in [SPAN] + list(range(1, SPAN)) for p in (SPAN - d, SPAN + d)] + [SPAN]

    for spot, place in enumerate(order):
        def fill_hot(n, carry, spot=spot, place=place):
            at = spot * lanes + n * lm
            hot[place * a_dev + n] = jnp.where(wide - tall == at, 1.0, 0.0).astype(bf16)
            return carry

        lax.fori_loop(0, a_dev, fill_hot, 0)
    hot[places * a_dev] = jnp.zeros((lm, places * lanes), bf16)

    row = lax.broadcasted_iota(jnp.int32, (lanes, lanes), 0)
    col = lax.broadcasted_iota(jnp.int32, (lanes, lanes), 1)
    row_block, col_block = row // lm, col // lm
    same = row_block == col_block
    spread = jnp.where(row - row_block * lm == col - col_block * lm, 1.0, 0.0).astype(bf16)

    def diagonal(block):
        return jnp.where(same, jnp.concatenate([block] * a_dev, axis=0), 0.0).astype(bf16)

    tile = min(256, dim)
    unit = lax.broadcasted_iota(jnp.int32, (tile, tile), 0) == lax.broadcasted_iota(jnp.int32, (tile, tile), 1)
    unit = jnp.where(unit, 1.0, 0.0).astype(bf16)

    def turn_one(a):
        pltpu.make_async_copy(s_hbm.at[a], s_v.at[a], s_sem.at[a]).wait()
        for c in range(dim // tile):
            left = unit
            if c == 0:
                start = jnp.concatenate([firstx[a], jnp.zeros((lm, tile - lanes), f32)], axis=1)
                left = jnp.concatenate([unit, start.astype(bf16)], axis=0)
            got = mm(left, s_v[a, :, c * tile:(c + 1) * tile], NT).astype(bf16)
            s_t[a, c * tile:(c + 1) * tile, :] = got[:tile]
            if c == 0:
                img[a] = got[tile:]

    def turn(pair, carry):
        turn_one(2 * pair)
        turn_one(2 * pair + 1)
        return carry

    lax.fori_loop(0, a_dev // 4, turn, 0)

    for copy in t_copies:
        copy.wait()
    t_all[SPAN] = t_turned
    i_copy.wait()

    for place in range(places):
        block = mm(diagonal(t_all[place]), spread).astype(bf16)
        table[pl.ds(place * a_dev, a_dev)] = block.reshape(a_dev, lm, lanes)
    table[places * a_dev] = jnp.zeros((lm, lanes), bf16)

    def fill_bd(a, carry):
        for s in range(zone):
            tile = table[idx_s[a, s]]
            keep = lane16 // lm == s % per
            bd[a, pl.ds(s * lm, lm), :] = jnp.where(keep, tile.astype(f32), 0.0).astype(bf16)
        return carry

    lax.fori_loop(0, a_dev, fill_bd, 0)

    lax.fori_loop(a_dev // 4, a_dev // 2, turn, 0)

    def sweep(step, carry):
        for a in range(a_dev):
            parts = []
            for g in range(n_groups):
                part = mm(img[a, :, g * lanes:(g + 1) * lanes], bd[a, g * lanes:(g + 1) * lanes, :])
                if g == 0:
                    part = part + firstx[a]
                parts.append(part.astype(bf16))
            flat = jnp.concatenate(parts, axis=1)
            img[a] = mm(flat, s_t[a]).astype(bf16)
        return carry

    lax.fori_loop(0, ITERS - 1, sweep, 0)

    def send_acc(d):
        return pltpu.make_async_remote_copy(
            src_ref=acc.at[SPAN + d], dst_ref=landed.at[SPAN - d], send_sem=as_sem.at[SPAN - d],
            recv_sem=ar_sem.at[SPAN - d], device_id={"atom": atom_at(d)}, device_id_type=pl.DeviceIdType.MESH,
        )

    slots = 16
    chunk = slots * lm
    a_copies = []
    for lo in range(0, places, 2):
        here = order[lo:lo + 2]
        columns = slice(lo * lanes, (lo + len(here)) * lanes)
        whole = None
        for a in range(a_dev):
            for g in range(zone // slots):
                rows = [idx_s[a, g * slots + s] for s in range(slots)]
                right = jnp.concatenate([hot[r, :, columns] for r in rows], axis=0)
                got = mm(img[a, :, g * chunk:(g + 1) * chunk], right)
                whole = got if whole is None else whole + got
        for n, place in enumerate(here):
            acc[place] = whole[:, n * lanes:(n + 1) * lanes]
            if place != SPAN:
                copy = send_acc(place - SPAN)
                copy.start()
                a_copies.append(copy)
    r_copy.wait()
    own = diagonal(t_turned)
    for copy in a_copies:
        copy.wait()
    gathered = acc[SPAN]
    for d in shifts:
        gathered = gathered + landed[SPAN - d]
    high = gathered.astype(bf16)
    low = (gathered - high.astype(f32)).astype(bf16)
    received = t_turned + (mm(high, own) + mm(low, own))
    turned = mm(diagonal(received.astype(bf16).astype(f32)), r_v[...])
    products = turned * r_v[...].astype(f32)
    density = jnp.sum(products.reshape(a_dev, lm, products.shape[1]), axis=1) * w_ref[0]
    share = density.shape[1] // n_energy
    for q in range(n_energy):
        d_mine[q] = density[:, q * share:(q + 1) * share]

    def send_d(d):
        to = lax.rem(my_e + d, n_energy)
        return pltpu.make_async_remote_copy(
            src_ref=d_mine.at[to], dst_ref=d_land.at[d - 1], send_sem=ds_sem.at[d - 1],
            recv_sem=dr_sem.at[d - 1], device_id={"energy": to}, device_id_type=pl.DeviceIdType.MESH,
        )

    d_copies = [send_d(d) for d in range(1, n_energy)]
    for copy in d_copies:
        copy.start()
    for copy in d_copies:
        copy.wait()
    result = d_mine[my_e]
    for d in range(1, n_energy):
        result = result + d_land[d - 1]
    out_ref[...] = result


def shards(n_atom, n_energy, t_matrix, structure, radial, weights, neighbours, live):
    _, a_dev, lm, _ = t_matrix.shape
    zone = neighbours.shape[1]
    mesh_points = radial.shape[-1]
    dim, lanes, places = zone * lm, a_dev * lm, 2 * SPAN + 1
    share = mesh_points // n_energy
    vmem = pl.BlockSpec(memory_space=pltpu.VMEM)
    hbm = pl.BlockSpec(memory_space=pltpu.HBM)
    f32, bf16 = jnp.float32, jnp.bfloat16
    dma = pltpu.SemaphoreType.DMA
    return pl.pallas_call(
        functools.partial(kernel, n_atom, n_energy, a_dev, lm, zone),
        out_shape=jax.ShapeDtypeStruct((a_dev, share), f32),
        in_specs=[hbm] * 6,
        out_specs=vmem,
        scratch_shapes=[
            pltpu.VMEM((lanes, lm), f32),
            pltpu.SMEM((1,), f32),
            pltpu.VMEM((a_dev, zone), jnp.int32),
            pltpu.VMEM((a_dev, zone), jnp.int32),
            pltpu.VMEM((a_dev, dim, dim), bf16),
            pltpu.VMEM((a_dev, dim, dim), bf16),
            pltpu.VMEM((lanes, mesh_points), bf16),
            pltpu.VMEM((lm, lanes), f32),
            pltpu.VMEM((places, lm, lanes), f32),
            pltpu.VMEM((a_dev, lm, lanes), f32),
            pltpu.VMEM((places * a_dev + 1, lm, lanes), bf16),
            pltpu.VMEM((places * a_dev + 1, lm, places * lanes), bf16),
            pltpu.VMEM((a_dev, dim, lanes), bf16),
            pltpu.VMEM((a_dev, lm, dim), bf16),
            pltpu.VMEM((a_dev, zone), jnp.int32),
            pltpu.SMEM((a_dev, zone), jnp.int32),
            pltpu.VMEM((places, lm, lanes), f32),
            pltpu.VMEM((places, lm, lanes), f32),
            pltpu.VMEM((n_energy, a_dev, share), f32),
            pltpu.VMEM((n_energy, a_dev, share), f32),
            dma((a_dev,)),
            dma((6,)),
            dma((places,)),
            dma((places,)),
            dma((places,)),
            dma((places,)),
            dma((n_energy,)),
            dma((n_energy,)),
        ],
        compiler_params=pltpu.CompilerParams(collective_id=0, has_side_effects=True, vmem_limit_bytes=56 * 1024 * 1024),
        name="tau_density",
    )(
        t_matrix.reshape(lanes, lm),
        structure.reshape(a_dev, dim, dim),
        radial.reshape(lanes, mesh_points),
        weights,
        neighbours,
        live,
    )


def solution(mesh):
    in_specs = (
        P("energy", "atom", None, None),
        P("energy", "atom", None, None),
        P("energy", "atom", None, None),
        P("energy"),
        P("atom", None),
        P("atom", None),
    )
    out_specs = P("atom", "energy")
    body = functools.partial(shards, mesh.shape["atom"], mesh.shape["energy"])
    return jax.shard_map(body, mesh=mesh, in_specs=in_specs, out_specs=out_specs, check_vma=False)
```

profile of v0, /device:TPU:0, one launch (start us, length us, event | category | flops | bytes accessed | tf_op | source)
XLA Modules:
  0.0 37.3 jit_solution(5813452780039170818)
XLA Ops:
  0.7 35.4 %tau_density.1 = f32[8,256]{1,0:T(8,128)} custom-call(f32[128,16]{1,0:T(8,128)} %bitcast.5, bf16[8,1024,1024]{2,1,0:T(8,128)(2,1)} %bitcast.3, bf16[128,1024]{1,0:T(8,128)(2,1)} %bitcast.4, f32[1]{0:T(128)S(6)} %copy.8.w_hbm, s32[8,64]{1,0:T(8,128)} %nb_hbm.1, s32[8,64]{1,0:T(8,128)} %live_hbm.1), custom_call_target="tpu_custom_call" | custom-call | tf_op jit(solution)/shard_map/tau_density/pallas_call | solution.py:242
  36.0 1.3 %copy.9 = f32[8,256]{1,0:T(8,128)} copy(f32[8,256]{1,0:T(8,128)} %tau_density.1) | data formatting | bytes 16384
where the time goes:
time: 37.6 us; the launch traced here: 37.3 us
  Pallas kernels  35.4 us (94%)
  local copies, waits for them, and re-layouts  1.3 us (3%)
  between operations  0.66 us (2%)
    pallas_call x1, Pallas kernels, shards(): pl.pallas_call(functools.partial(kernel, n_atom, n_energy, a_dev, lm, zon...  35.4 us
    unnamed x1, local copies, waits for them, and re-layouts  1.3 us

commit v1 on v0

v1 whole, which is shorter than its diff:
```python
import functools

import jax
import jax.numpy as jnp
from jax import lax
from jax.experimental import pallas as pl
from jax.experimental.pallas import tpu as pltpu
from jax.sharding import PartitionSpec as P

ITERS = 4
SPAN = 3

NT = (((1,), (1,)), ((), ()))
NN = (((1,), (0,)), ((), ()))


def mm(a, b, dims=NN):
    return lax.dot_general(a, b, dims, preferred_element_type=jnp.float32)


WAIT = 300


def in_order(jobs):
    users = {name: [] for name in jobs}
    for name, (_, deps, _) in jobs.items():
        for dep in deps:
            users[dep].append(name)
    rank = {}

    def rank_of(name):
        if name not in rank:
            rank[name] = jobs[name][0] + max((WAIT + rank_of(user) for user in users[name]), default=0)
        return rank[name]

    order, ready_at, clock = [], {name: 0 for name in jobs if not jobs[name][1]}, 0
    missing = {name: len(deps) for name, (_, deps, _) in jobs.items()}
    at = {name: 0 for name in jobs}
    while ready_at:
        now = [name for name, t in ready_at.items() if t <= clock]
        if not now:
            clock = min(ready_at.values())
            continue
        name = max(now, key=rank_of)
        del ready_at[name]
        clock += jobs[name][0]
        order.append(jobs[name][2])
        for user in users[name]:
            at[user] = max(at[user], clock + WAIT)
            missing[user] -= 1
            if missing[user] == 0:
                ready_at[user] = at[user]
    return order


def kernel(
    n_atom, n_energy, a_dev, lm, zone,
    t_hbm, s_hbm, r_hbm, w_hbm, nb_hbm, live_hbm, out_ref,
    t_ref, w_ref, nb_ref, live_ref, s_v, s_t, r_v, t_send, t_all, firstx, table, hot, bd, pick, mask, reach, x12, x3, v, v3, v4,
    idx_v, idx_s, acc, landed, d_mine, d_land,
    s_sem, misc_sem, ts_sem, tr_sem, as_sem, ar_sem, ds_sem, dr_sem,
):
    bf16, f32 = jnp.bfloat16, jnp.float32
    places = 2 * SPAN + 1
    lanes = a_dev * lm
    dim = zone * lm
    per = lanes // lm
    me = lax.axis_index("atom")
    my_e = lax.axis_index("energy")

    small = [
        pltpu.make_async_copy(source, target, misc_sem.at[2 + n])
        for n, (source, target) in enumerate(
            ((t_hbm, t_ref), (nb_hbm, nb_ref), (live_hbm, live_ref), (w_hbm, w_ref))
        )
    ]
    for copy in small:
        copy.start()
    tile = min(256, dim)
    blocks = dim // tile
    s_copies = [pltpu.make_async_copy(s_hbm.at[a], s_v.at[a], s_sem.at[a]) for a in range(a_dev)]
    for copy in s_copies:
        copy.start(priority=1)
    r_copy = pltpu.make_async_copy(r_hbm, r_v, misc_sem.at[0])
    r_copy.start(priority=1)

    def atom_at(d):
        return lax.rem(me + (d + n_atom), n_atom)

    shifts = [s * d for d in range(SPAN, 0, -1) for s in (-1, 1)]
    barrier = pltpu.get_barrier_semaphore()
    for d in shifts:
        pl.semaphore_signal(barrier, inc=1, device_id={"atom": atom_at(d)}, device_id_type=pl.DeviceIdType.MESH)
    for d in range(1, n_energy):
        pl.semaphore_signal(
            barrier, inc=1, device_id={"energy": lax.rem(my_e + d, n_energy)}, device_id_type=pl.DeviceIdType.MESH
        )

    for copy in small:
        copy.wait()
    t_turned = jnp.transpose(t_ref[...])
    t_send[...] = t_turned
    ids = nb_ref[...] - (me - SPAN) * a_dev
    total = n_atom * a_dev
    ids = jnp.where(ids < 0, ids + total, ids)
    ids = jnp.where(ids >= total, ids - total, ids)
    ids = jnp.where(live_ref[...] > 0, ids, places * a_dev)
    idx_v[...] = ids
    i_copy = pltpu.make_async_copy(idx_v, idx_s, misc_sem.at[1])
    i_copy.start()

    lane16 = lax.broadcasted_iota(jnp.int32, (lm, lanes), 1)
    row16 = lax.broadcasted_iota(jnp.int32, (lm, lanes), 0)
    for a in range(a_dev):
        moved = t_turned if a == 0 else pltpu.roll(t_turned, lanes - a * lm, 1)
        firstx[a] = jnp.where(lane16 < lm, moved, 0.0)

    place_of = jnp.zeros(ids.shape, f32)
    for p in range(1, places + 1):
        place_of = place_of + jnp.where(ids >= p * a_dev, 1.0, 0.0)
    wide = lax.broadcasted_iota(jnp.int32, (zone, dim), 1)
    tall = lax.broadcasted_iota(jnp.int32, (zone, dim), 0)
    widen = jnp.where((wide >= tall * lm) & (wide < tall * lm + lm), 1.0, 0.0).astype(bf16)
    spread_place = mm(place_of.astype(bf16), widen)
    for a in range(a_dev):
        reach[a] = jnp.broadcast_to(spread_place[a:a + 1], (lm, dim))

    for n in range(a_dev):
        one = jnp.where(lane16 - row16 == n * lm, 1.0, 0.0).astype(bf16)
        for p in range(places):
            hot[p * a_dev + n] = one
    hot[places * a_dev] = jnp.zeros((lm, lanes), bf16)

    row = lax.broadcasted_iota(jnp.int32, (lanes, lanes), 0)
    col = lax.broadcasted_iota(jnp.int32, (lanes, lanes), 1)
    row_block, col_block = row // lm, col // lm
    same = row_block == col_block
    spread = jnp.where(row - row_block * lm == col - col_block * lm, 1.0, 0.0).astype(bf16)

    def diagonal(block):
        return jnp.where(same, jnp.concatenate([block] * a_dev, axis=0), 0.0).astype(bf16)

    unit = lax.broadcasted_iota(jnp.int32, (tile, tile), 0) == lax.broadcasted_iota(jnp.int32, (tile, tile), 1)
    unit = jnp.where(unit, 1.0, 0.0).astype(bf16)
    start = jnp.zeros((lm, tile - lanes), f32)

    def left_of(a, c):
        if c > 0:
            return unit
        return jnp.concatenate([unit, jnp.concatenate([firstx[a], start], axis=1).astype(bf16)], axis=0)

    def turn_tile(a, c, rows):
        got = mm(left_of(a, c), s_v[a, rows, c * tile:(c + 1) * tile], NT).astype(bf16)
        s_t[a, c * tile:(c + 1) * tile, rows] = got[:tile]
        if c == 0:
            v[a, :, rows] = got[tile:]

    def fill_pick(a):
        for s in range(zone):
            pick[a, pl.ds(s * lm, lm), :] = hot[idx_s[a, s]]

    def turn(a, carry):
        pltpu.make_async_copy(s_hbm.at[a], s_v.at[a], s_sem.at[a]).wait()
        for c in range(blocks):
            turn_tile(a, c, slice(0, dim))
        for p in range(places):
            mask[a, p] = jnp.where(reach[a] == p, 1.0, 0.0).astype(bf16)
        return carry

    early = a_dev * 3 // 8
    lax.fori_loop(0, early, turn, 0)

    pl.semaphore_wait(barrier, len(shifts) + n_energy - 1)

    def send_t(d):
        return pltpu.make_async_remote_copy(
            src_ref=t_send, dst_ref=t_all.at[SPAN - d], send_sem=ts_sem.at[SPAN - d],
            recv_sem=tr_sem.at[SPAN - d], device_id={"atom": atom_at(d)}, device_id_type=pl.DeviceIdType.MESH,
        )

    t_copies = [send_t(d) for d in shifts]
    for copy in t_copies:
        copy.start()

    lax.fori_loop(early, a_dev, turn, 0)
    i_copy.wait()

    def fill_table(place, block):
        block = mm(diagonal(block), spread).astype(bf16)
        table[pl.ds(place * a_dev, a_dev)] = block.reshape(a_dev, lm, lanes)

    fill_table(SPAN, t_turned)
    table[places * a_dev] = jnp.zeros((lm, lanes), bf16)
    for copy in t_copies:
        copy.wait()
    for d in shifts:
        fill_table(SPAN - d, t_all[SPAN - d])

    keep = [jnp.where(lane16 // lm == b, 1.0, 0.0).astype(bf16) for b in range(per)]

    def fill_bd(a):
        for s in range(zone):
            bd[a, pl.ds(s * lm, lm), :] = table[idx_s[a, s]] * keep[s % per]

    def column(a, r):
        parts = []
        for g in range(r * tile // lanes, (r + 1) * tile // lanes):
            at = slice(g * lanes, (g + 1) * lanes)
            part = mm(v[a, :, at], bd[a, at, :])
            if g == 0:
                part = part + firstx[a]
            parts.append(part.astype(bf16))
        return jnp.concatenate(parts, axis=1)

    def cols(lo, hi):
        return slice(lo * tile, hi * tile)

    def start_columns(a):
        for r in range(blocks):
            x12[a, :lm, cols(r, r + 1)] = column(a, r)

    def sweep_a(a, r):
        here = cols(r, r + 1)
        got = mm(x12[a, :lm, cols(r, blocks)], s_t[a, cols(r, blocks), here])
        if r > 0:
            both = mm(x12[a, :, cols(0, r)], s_t[a, cols(0, r), here])
            got = got + both[:lm]
            v3[a, :, here] = both[lm:]
        v[a, :, here] = got.astype(bf16)

    def column_a(a, r):
        got = column(a, r)
        x12[a, lm:, cols(r, r + 1)] = got
        x3[a, :lm, cols(r, r + 1)] = got

    def sweep_b(a, r):
        here = cols(r, r + 1)
        got = mm(x3[a, :lm, cols(r, r + 1)], s_t[a, here, here])
        if r + 1 < blocks:
            both = mm(x3[a, :, cols(r + 1, blocks)], s_t[a, cols(r + 1, blocks), here])
            got = got + both[:lm]
            v4[a, :, here] = both[lm:]
        if r > 0:
            got = got + v3[a, :, here]
        v[a, :, here] = got.astype(bf16)

    def column_b(a, r):
        x3[a, lm:, cols(r, r + 1)] = column(a, r)

    def sweep_c(a, r):
        here = cols(r, r + 1)
        got = mm(x3[a, lm:, cols(0, r + 1)], s_t[a, cols(0, r + 1), here])
        if r + 1 < blocks:
            got = got + v4[a, :, here]
        v[a, :, here] = got.astype(bf16)

    whole = [None]

    def scatter(a, r):
        here = cols(r, r + 1)
        block = v[a, :, here]
        left = jnp.concatenate([block * mask[a, p, :, here] for p in range(places)], axis=0)
        got = mm(left, pick[a, here, :])
        whole[0] = got if whole[0] is None else whole[0] + got

    step = tile // 8
    jobs = {}

    def job(name, cost, deps, fn, *args):
        jobs[name] = (cost, deps, functools.partial(fn, *args))

    for a in range(a_dev):
        job(("f", a), 2 * step, [], fill_bd, a)
        job(("p", a), 0, [("z", a)], fill_pick, a)
        job(("z", a), blocks * step, [("f", a)], start_columns, a)
        for r in range(blocks):
            job(("a", a, r), blocks * step, [("z", a)] + [("ca", a, c) for c in range(r)], sweep_a, a, r)
            job(("ca", a, r), step, [("a", a, r)], column_a, a, r)
            later = range(r + 1, blocks)
            job(("b", a, r), (blocks - r) * step, [("ca", a, r)] + [("cb", a, c) for c in later], sweep_b, a, r)
            job(("cb", a, r), step, [("b", a, r)], column_b, a, r)
            job(("c", a, r), (r + 1) * step, [("cb", a, c) for c in range(r + 1)], sweep_c, a, r)
            job(("s", a, r), step, [("c", a, r), ("p", a)], scatter, a, r)
    for fn in in_order(jobs):
        fn()

    def send_acc(d):
        return pltpu.make_async_remote_copy(
            src_ref=acc.at[SPAN + d], dst_ref=landed.at[SPAN - d], send_sem=as_sem.at[SPAN - d],
            recv_sem=ar_sem.at[SPAN - d], device_id={"atom": atom_at(d)}, device_id_type=pl.DeviceIdType.MESH,
        )

    for p in range(places):
        acc[p] = whole[0][p * lm:(p + 1) * lm]
    a_copies = [send_acc(d) for d in shifts]
    for copy in a_copies:
        copy.start()
    r_copy.wait()
    own = diagonal(t_turned)
    for copy in a_copies:
        copy.wait()
    gathered = acc[SPAN]
    for d in shifts:
        gathered = gathered + landed[SPAN - d]
    high = gathered.astype(bf16)
    low = (gathered - high.astype(f32)).astype(bf16)
    received = t_turned + (mm(high, own) + mm(low, own))
    turned = mm(diagonal(received.astype(bf16).astype(f32)), r_v[...])
    products = turned * r_v[...].astype(f32)
    density = jnp.sum(products.reshape(a_dev, lm, products.shape[1]), axis=1) * w_ref[0]
    share = density.shape[1] // n_energy
    for q in range(n_energy):
        d_mine[q] = density[:, q * share:(q + 1) * share]

    def send_d(d):
        to = lax.rem(my_e + d, n_energy)
        return pltpu.make_async_remote_copy(
            src_ref=d_mine.at[to], dst_ref=d_land.at[d - 1], send_sem=ds_sem.at[d - 1],
            recv_sem=dr_sem.at[d - 1], device_id={"energy": to}, device_id_type=pl.DeviceIdType.MESH,
        )

    d_copies = [send_d(d) for d in range(1, n_energy)]
    for copy in d_copies:
        copy.start()
    for copy in d_copies:
        copy.wait()
    result = d_mine[my_e]
    for d in range(1, n_energy):
        result = result + d_land[d - 1]
    out_ref[...] = result


def shards(n_atom, n_energy, t_matrix, structure, radial, weights, neighbours, live):
    _, a_dev, lm, _ = t_matrix.shape
    zone = neighbours.shape[1]
    mesh_points = radial.shape[-1]
    dim, lanes, places = zone * lm, a_dev * lm, 2 * SPAN + 1
    share = mesh_points // n_energy
    vmem = pl.BlockSpec(memory_space=pltpu.VMEM)
    hbm = pl.BlockSpec(memory_space=pltpu.HBM)
    f32, bf16 = jnp.float32, jnp.bfloat16
    dma = pltpu.SemaphoreType.DMA
    pin = functools.partial(pltpu.with_memory_space_constraint, memory_space=pltpu.HBM)
    return pl.pallas_call(
        functools.partial(kernel, n_atom, n_energy, a_dev, lm, zone),
        out_shape=jax.ShapeDtypeStruct((a_dev, share), f32),
        in_specs=[hbm] * 6,
        out_specs=vmem,
        scratch_shapes=[
            pltpu.VMEM((lanes, lm), f32),
            pltpu.SMEM((1,), f32),
            pltpu.VMEM((a_dev, zone), jnp.int32),
            pltpu.VMEM((a_dev, zone), jnp.int32),
            pltpu.VMEM((a_dev, dim, dim), bf16),
            pltpu.VMEM((a_dev, dim, dim), bf16),
            pltpu.VMEM((lanes, mesh_points), bf16),
            pltpu.VMEM((lm, lanes), f32),
            pltpu.VMEM((places, lm, lanes), f32),
            pltpu.VMEM((a_dev, lm, lanes), f32),
            pltpu.VMEM((places * a_dev + 1, lm, lanes), bf16),
            pltpu.VMEM((places * a_dev + 1, lm, lanes), bf16),
            pltpu.VMEM((a_dev, dim, lanes), bf16),
            pltpu.VMEM((a_dev, dim, lanes), bf16),
            pltpu.VMEM((a_dev, places, lm, dim), bf16),
            pltpu.VMEM((a_dev, lm, dim), f32),
            pltpu.VMEM((a_dev, 2 * lm, dim), bf16),
            pltpu.VMEM((a_dev, 2 * lm, dim), bf16),
            pltpu.VMEM((a_dev, lm, dim), bf16),
            pltpu.VMEM((a_dev, lm, dim), f32),
            pltpu.VMEM((a_dev, lm, dim), f32),
            pltpu.VMEM((a_dev, zone), jnp.int32),
            pltpu.SMEM((a_dev, zone), jnp.int32),
            pltpu.VMEM((places, lm, lanes), f32),
            pltpu.VMEM((places, lm, lanes), f32),
            pltpu.VMEM((n_energy, a_dev, share), f32),
            pltpu.VMEM((n_energy, a_dev, share), f32),
            dma((a_dev,)),
            dma((6,)),
            dma((places,)),
            dma((places,)),
            dma((places,)),
            dma((places,)),
            dma((n_energy,)),
            dma((n_energy,)),
        ],
        compiler_params=pltpu.CompilerParams(collective_id=0, has_side_effects=True, vmem_limit_bytes=52 * 1024 * 1024),
        name="tau_density",
    )(
        pin(t_matrix.reshape(lanes, lm)),
        pin(structure.reshape(a_dev, dim, dim)),
        pin(radial.reshape(lanes, mesh_points)),
        weights,
        pin(neighbours),
        pin(live),
    )


def solution(mesh):
    in_specs = (
        P("energy", "atom", None, None),
        P("energy", "atom", None, None),
        P("energy", "atom", None, None),
        P("energy"),
        P("atom", None),
        P("atom", None),
    )
    out_specs = P("atom", "energy")
    body = functools.partial(shards, mesh.shape["atom"], mesh.shape["energy"])
    return jax.shard_map(body, mesh=mesh, in_specs=in_specs, out_specs=out_specs, check_vma=False)
```

time: 37.6 us -> 30.3 us (0.81)
  Pallas kernels: 35.4 us -> 28.9 us
  local copies, waits for them, and re-layouts: 1.3 us -> 0.6 us
    pallas_call x1, Pallas kernels: 35.4 us -> 28.9 us  [shards(): pl.pallas_call(functools.partial(kernel, n_atom, n_energy, a_dev, lm, zon...]
    unnamed x1, local copies, waits for them, and re-layouts: 1.3 us -> 0.6 us
where the time goes in v1:
time: 30.3 us; the launch traced here: 30.2 us
  Pallas kernels  28.9 us (95%)
  between operations  0.66 us (2%)
  local copies, waits for them, and re-layouts  0.6 us (2%)
    pallas_call x1, Pallas kernels, shards(): pl.pallas_call(functools.partial(kernel, n_atom, n_energy, a_dev, lm, zon...  28.9 us

profile of v1, /device:TPU:0, one launch (start us, length us, event | category | flops | bytes accessed | tf_op | source)
XLA Modules:
  0.0 30.2 jit_solution(17656468907452919963)
XLA Ops:
  0.7 28.9 %tau_density.1 = f32[8,256]{1,0:T(8,128)S(1)} custom-call(f32[128,16]{1,0:T(8,128)} %bitcast.5, bf16[8,1024,1024]{2,1,0:T(8,128)(2,1)} %bitcast.3, bf16[128,1024]{1,0:T(8,128)(2,1)} %bitcast.4, f32[1]{0:T(128)S(6)} %copy.8.w_hbm, s32[8,64]{1,0:T(8,128)} %nb_hbm.1, s32[8,64]{1,0:T(8,128)} %live_hbm.1), custom_call_target="tpu_custom_call" | custom-call | tf_op jit(solution)/shard_map/tau_density/pallas_call | solution.py:344
  29.6 0.6 %copy.9 = f32[8,256]{1,0:T(8,128)} copy(f32[8,256]{1,0:T(8,128)S(1)} %tau_density.1) | data formatting | bytes 16384

commit v2 on v1

--- a/solution.py
+++ b/solution.py
@@ -56,7 +56,7 @@
 def kernel(
     n_atom, n_energy, a_dev, lm, zone,
     t_hbm, s_hbm, r_hbm, w_hbm, nb_hbm, live_hbm, out_ref,
-    t_ref, w_ref, nb_ref, live_ref, s_v, s_t, r_v, t_send, t_all, firstx, table, hot, bd, pick, mask, reach, x12, x3, v, v3, v4,
+    t_ref, w_ref, nb_ref, live_ref, s_v, s_t, r_v, t_send, t_all, firstx, table, hot, bd, pick, mask, reach, x12, x3, v, v3, v4, share,
     idx_v, idx_s, acc, landed, d_mine, d_land,
     s_sem, misc_sem, ts_sem, tr_sem, as_sem, ar_sem, ds_sem, dr_sem,
 ):
@@ -167,7 +167,8 @@
             mask[a, p] = jnp.where(reach[a] == p, 1.0, 0.0).astype(bf16)
         return carry
 
-    early = a_dev * 3 // 8
+    early = a_dev // 4
+    turned_first = a_dev - a_dev * 3 // 8
     lax.fori_loop(0, early, turn, 0)
 
     pl.semaphore_wait(barrier, len(shifts) + n_energy - 1)
@@ -182,7 +183,17 @@
     for copy in t_copies:
         copy.start()
 
-    lax.fori_loop(early, a_dev, turn, 0)
+    def begin(a, carry):
+        pltpu.make_async_copy(s_hbm.at[a], s_v.at[a], s_sem.at[a]).wait()
+        got = mm(firstx[a].astype(bf16), s_v[a, :, :lanes], NT)
+        v4[a] = got
+        v[a] = got.astype(bf16)
+        for p in range(places):
+            mask[a, p] = jnp.where(reach[a] == p, 1.0, 0.0).astype(bf16)
+        return carry
+
+    lax.fori_loop(early, turned_first, turn, 0)
+    lax.fori_loop(turned_first, a_dev, begin, 0)
     i_copy.wait()
 
     def fill_table(place, block):
@@ -200,17 +211,19 @@
 
     def fill_bd(a):
         for s in range(zone):
-            bd[a, pl.ds(s * lm, lm), :] = table[idx_s[a, s]] * keep[s % per]
+            g = s // per
+            at = g // 2 * lanes + s % per * lm
+            half = slice(g % 2 * lanes, (g % 2 + 1) * lanes)
+            bd[a, at:at + lm, half] = table[idx_s[a, s]] * keep[s % per]
 
     def column(a, r):
-        parts = []
-        for g in range(r * tile // lanes, (r + 1) * tile // lanes):
-            at = slice(g * lanes, (g + 1) * lanes)
-            part = mm(v[a, :, at], bd[a, at, :])
-            if g == 0:
-                part = part + firstx[a]
-            parts.append(part.astype(bf16))
-        return jnp.concatenate(parts, axis=1)
+        halves = [slice(h * lanes, (h + 1) * lanes) for h in range(2)]
+        left = jnp.concatenate([v[a, :, r * tile + h * lanes:r * tile + (h + 1) * lanes] for h in range(2)], axis=0)
+        both = mm(left, bd[a, r * lanes:(r + 1) * lanes, :])
+        parts = [both[h * lm:(h + 1) * lm, halves[h]] for h in range(2)]
+        if r == 0:
+            parts[0] = parts[0] + firstx[a]
+        return jnp.concatenate([part.astype(bf16) for part in parts], axis=1)
 
     def cols(lo, hi):
         return slice(lo * tile, hi * tile)
@@ -254,6 +267,41 @@
             got = got + v4[a, :, here]
         v[a, :, here] = got.astype(bf16)
 
+    void = jnp.zeros((lanes, lanes), bf16)
+
+    def fold(a, c):
+        rows = []
+        for g in range(2):
+            block = bd[a, c * lanes:(c + 1) * lanes, g * lanes:(g + 1) * lanes]
+            rows.append(jnp.concatenate([block, void] if g == 0 else [void, block], axis=1))
+        left = jnp.concatenate(rows + [x12[a, :lm, cols(c, c + 1)]], axis=0)
+        got = mm(left, s_v[a, :, cols(c, c + 1)], NT)
+        s_t[a, cols(c, c + 1), :] = got[:tile].astype(bf16)
+        share[a - turned_first, c] = got[tile:]
+
+    def gather(a):
+        got = share[a - turned_first, 0]
+        for c in range(1, blocks):
+            got = got + share[a - turned_first, c]
+        x12[a, :lm, :] = got.astype(bf16)
+
+    def fold_a(a, r):
+        here = cols(r, r + 1)
+        got = mm(x12[a, :lm, cols(r, blocks)], s_t[a, cols(r, blocks), here]) + v4[a, :, here]
+        if r > 0:
+            both = mm(x12[a, :, cols(0, r)], s_t[a, cols(0, r), here])
+            got = got + both[:lm]
+            v3[a, :, here] = both[lm:]
+        x12[a, lm:, here] = got.astype(bf16)
+        x3[a, :lm, here] = got.astype(bf16)
+
+    def fold_b(a, r):
+        here = cols(r, r + 1)
+        got = mm(x3[a, :lm, cols(r, blocks)], s_t[a, cols(r, blocks), here]) + v4[a, :, here]
+        if r > 0:
+            got = got + v3[a, :, here]
+        v[a, :, here] = got.astype(bf16)
+
     whole = [None]
 
     def scatter(a, r):
@@ -272,13 +320,22 @@
     for a in range(a_dev):
         job(("f", a), 2 * step, [], fill_bd, a)
         job(("p", a), 0, [("z", a)], fill_pick, a)
-        job(("z", a), blocks * step, [("f", a)], start_columns, a)
+        job(("z", a), blocks * step // 2, [("f", a)], start_columns, a)
+        if a >= turned_first:
+            for c in range(blocks):
+                job(("g", a, c), 9 * blocks * step // 4, [("z", a)], fold, a, c)
+            job(("h", a), 0, [("g", a, c) for c in range(blocks)], gather, a)
+            for r in range(blocks):
+                job(("a", a, r), blocks * step, [("h", a)] + [("a", a, c) for c in range(r)], fold_a, a, r)
+                job(("c", a, r), (blocks - r) * step, [("a", a, c) for c in range(r, blocks)], fold_b, a, r)
+                job(("s", a, r), step, [("c", a, r), ("p", a)], scatter, a, r)
+            continue
         for r in range(blocks):
             job(("a", a, r), blocks * step, [("z", a)] + [("ca", a, c) for c in range(r)], sweep_a, a, r)
-            job(("ca", a, r), step, [("a", a, r)], column_a, a, r)
+            job(("ca", a, r), step // 2, [("a", a, r)], column_a, a, r)
             later = range(r + 1, blocks)
             job(("b", a, r), (blocks - r) * step, [("ca", a, r)] + [("cb", a, c) for c in later], sweep_b, a, r)
-            job(("cb", a, r), step, [("b", a, r)], column_b, a, r)
+            job(("cb", a, r), step // 2, [("b", a, r)], column_b, a, r)
             job(("c", a, r), (r + 1) * step, [("cb", a, c) for c in range(r + 1)], sweep_c, a, r)
             job(("s", a, r), step, [("c", a, r), ("p", a)], scatter, a, r)
     for fn in in_order(jobs):
@@ -308,9 +365,9 @@
     turned = mm(diagonal(received.astype(bf16).astype(f32)), r_v[...])
     products = turned * r_v[...].astype(f32)
     density = jnp.sum(products.reshape(a_dev, lm, products.shape[1]), axis=1) * w_ref[0]
-    share = density.shape[1] // n_energy
+    part = density.shape[1] // n_energy
     for q in range(n_energy):
-        d_mine[q] = density[:, q * share:(q + 1) * share]
+        d_mine[q] = density[:, q * part:(q + 1) * part]
 
     def send_d(d):
         to = lax.rem(my_e + d, n_energy)
@@ -359,7 +416,7 @@
             pltpu.VMEM((a_dev, lm, lanes), f32),
             pltpu.VMEM((places * a_dev + 1, lm, lanes), bf16),
             pltpu.VMEM((places * a_dev + 1, lm, lanes), bf16),
-            pltpu.VMEM((a_dev, dim, lanes), bf16),
+            pltpu.VMEM((a_dev, dim // 2, 2 * lanes), bf16),
             pltpu.VMEM((a_dev, dim, lanes), bf16),
             pltpu.VMEM((a_dev, places, lm, dim), bf16),
             pltpu.VMEM((a_dev, lm, dim), f32),
@@ -368,6 +425,7 @@
             pltpu.VMEM((a_dev, lm, dim), bf16),
             pltpu.VMEM((a_dev, lm, dim), f32),
             pltpu.VMEM((a_dev, lm, dim), f32),
+            pltpu.VMEM((a_dev * 3 // 8, dim // min(256, dim), lm, dim), f32),
             pltpu.VMEM((a_dev, zone), jnp.int32),
             pltpu.SMEM((a_dev, zone), jnp.int32),
             pltpu.VMEM((places, lm, lanes), f32),

time: 30.3 us -> 29.2 us (0.964)
  Pallas kernels: 28.9 us -> 27.8 us
    pallas_call x1, Pallas kernels: 28.9 us -> 27.8 us  [shards(): pl.pallas_call(functools.partial(kernel, n_atom, n_energy, a_dev, lm, zon...]
where the time goes in v2:
time: 29.2 us; the launch traced here: 29.1 us
  Pallas kernels  27.8 us (95%)
  between operations  0.66 us (2%)
  local copies, waits for them, and re-layouts  0.6 us (2%)
    pallas_call x1, Pallas kernels, shards(): pl.pallas_call(functools.partial(kernel, n_atom, n_energy, a_dev, lm, zon...  27.8 us
    unnamed x1, local copies, waits for them, and re-layouts  0.6 us

profile of v2, /device:TPU:0, one launch (start us, length us, event | category | flops | bytes accessed | tf_op | source)
XLA Modules:
  0.0 29.1 jit_solution(10564217318958282282)
XLA Ops:
  0.7 27.8 %tau_density.1 = f32[8,256]{1,0:T(8,128)S(1)} custom-call(f32[128,16]{1,0:T(8,128)} %bitcast.5, bf16[8,1024,1024]{2,1,0:T(8,128)(2,1)} %bitcast.3, bf16[128,1024]{1,0:T(8,128)(2,1)} %bitcast.4, f32[1]{0:T(128)S(6)} %copy.8.w_hbm, s32[8,64]{1,0:T(8,128)} %nb_hbm.1, s32[8,64]{1,0:T(8,128)} %live_hbm.1), custom_call_target="tpu_custom_call" | custom-call | tf_op jit(solution)/shard_map/tau_density/pallas_call | solution.py:401
  28.5 0.6 %copy.9 = f32[8,256]{1,0:T(8,128)} copy(f32[8,256]{1,0:T(8,128)S(1)} %tau_density.1) | data formatting | bytes 16384

commit v3 on v2

--- a/solution.py
+++ b/solution.py
@@ -349,7 +349,7 @@
 
     for p in range(places):
         acc[p] = whole[0][p * lm:(p + 1) * lm]
-    a_copies = [send_acc(d) for d in shifts]
+    a_copies = [send_acc(d) for d in reversed(shifts)]
     for copy in a_copies:
         copy.start()
     r_copy.wait()

time: 29.2 us -> 28.9 us (0.990)
  Pallas kernels: 27.8 us -> 27.5 us
    pallas_call x1, Pallas kernels: 27.8 us -> 27.5 us  [shards(): pl.pallas_call(functools.partial(kernel, n_atom, n_energy, a_dev, lm, zon...]
where the time goes in v3:
time: 28.9 us; the launch traced here: 28.7 us
  Pallas kernels  27.5 us (95%)
  between operations  0.66 us (2%)
  local copies, waits for them, and re-layouts  0.6 us (2%)
    pallas_call x1, Pallas kernels, shards(): pl.pallas_call(functools.partial(kernel, n_atom, n_energy, a_dev, lm, zon...  27.5 us
    unnamed x1, local copies, waits for them, and re-layouts  0.6 us

profile of v3, /device:TPU:0, one launch (start us, length us, event | category | flops | bytes accessed | tf_op | source)
XLA Modules:
  0.0 28.7 jit_solution(286552213344130705)
XLA Ops:
  0.7 27.5 %tau_density.1 = f32[8,256]{1,0:T(8,128)S(1)} custom-call(f32[128,16]{1,0:T(8,128)} %bitcast.5, bf16[8,1024,1024]{2,1,0:T(8,128)(2,1)} %bitcast.3, bf16[128,1024]{1,0:T(8,128)(2,1)} %bitcast.4, f32[1]{0:T(128)S(6)} %copy.8.w_hbm, s32[8,64]{1,0:T(8,128)} %nb_hbm.1, s32[8,64]{1,0:T(8,128)} %live_hbm.1), custom_call_target="tpu_custom_call" | custom-call | tf_op jit(solution)/shard_map/tau_density/pallas_call | solution.py:401
  28.1 0.6 %copy.9 = f32[8,256]{1,0:T(8,128)} copy(f32[8,256]{1,0:T(8,128)S(1)} %tau_density.1) | data formatting | bytes 16384
